TPU v7x, 32 devices: a whole 2x2x4 slice. The times are simulated.
32 devices in a mesh: dp: 4 (over y, x), expert: 8 (over z, core).
Axes of the slice: x: 2, y: 2, z: 4, core: 2. Of those that a mesh axis runs over, the one named last changes fastest.
Arguments:
- tokens: bfloat16 [4096, 2048], P(('dp', 'expert')), may hold values from -6 to 6
- expert_ids: int32 [4096, 2], P(('dp', 'expert')), may hold values from 0 to 7, all different within a row; in each aligned block of 128 rows (0 to 127, 128 to 255, ...) at most 40 rows name the same one
- gate_units: int32 [4096, 2], P(('dp', 'expert')), may hold values from 64 to 1023
- capacity: int32 [8], replicated, may hold values from 512 to 1535
- w_gate: bfloat16 [8, 2048, 1408], P('expert', None, 'dp'), may hold values from -0.125 to 0.125
- w_up: bfloat16 [8, 2048, 1408], P('expert', None, 'dp'), may hold values from -0.125 to 0.125
- w_down: bfloat16 [8, 2048, 1408], P('expert', None, 'dp'), may hold values from -0.15625 to 0.15625
Outputs:
- mixed: bfloat16 [4096, 2048], P(('dp', 'expert'))
Inputs may be any that keep to these rules, and one draw needn't show every extreme that they name: `expert_ids`: each row names two different experts; of one device's 128 rows (aligned blocks) no expert is named more than 40 times.
All inputs are finite; a program needn't handle non-finite values.
Results may differ from a plain program's by a relative error of at most 0.0057.
Values may be sent and summed in bfloat16 or wider, within the bound.
A program may use at most 128 MiB of HBM per device.

v0:
```python
import jax
import jax.numpy as jnp
from jax import lax
from jax.sharding import PartitionSpec as P


def prefix(shard, axis, combine, identity):
    length, here = (lax.axis_size(axis), lax.axis_index(axis))
    everything = lax.all_gather(shard, axis)
    start = jnp.broadcast_to(jnp.asarray(identity, shard.dtype), shard.shape)

    def step(k, before):
        reached = k < here
        new = combine(before, everything[k])
        return jnp.where(reached, new, before)

    return lax.fori_loop(0, length, step, start)


def expert_rows(rows, gate_w, up_w, down_w):
    gate = jnp.dot(rows, gate_w, preferred_element_type=jnp.float32)
    up = jnp.dot(rows, up_w, preferred_element_type=jnp.float32)
    hidden = (jax.nn.silu(gate) * up).astype(jnp.bfloat16)
    return lax.dot_general(
        hidden, down_w, (((1,), (1,)), ((), ())), preferred_element_type=jnp.float32
    )


def add_counts(earlier, later):
    return earlier + later


def local(tokens, expert_ids, gate_units, capacity, w_gate, w_up, w_down):
    tok_rows = tokens.shape[0]
    width = tokens.shape[1]
    n_experts = capacity.shape[0]
    most = max(2, 5 * tok_rows // (2 * n_experts))
    slots_all = n_experts * most
    flat = expert_ids.reshape(-1)
    onehot = (flat[:, None] == jnp.arange(n_experts, dtype=jnp.int32)[None, :]).astype(jnp.int32)
    local_rank = jnp.sum((jnp.cumsum(onehot, axis=0) - onehot) * onehot, axis=1)
    counts = jnp.sum(onehot, axis=0)
    offsets = prefix(counts, ("dp", "expert"), add_counts, jnp.zeros_like(counts))
    global_slot = jnp.sum(onehot * offsets[None, :], axis=1) + local_rank
    limit = jnp.sum(onehot * capacity[None, :], axis=1)
    kept = global_slot < limit
    weight = jnp.where(kept, gate_units.reshape(-1).astype(jnp.float32) / 1024.0, jnp.float32(0.0))
    send_slot = flat * most + local_rank
    chosen = (send_slot[None, :] == jnp.arange(slots_all, dtype=jnp.int32)[:, None]) & kept[None, :]
    placing = jnp.sum(chosen.reshape(slots_all, tok_rows, 2).astype(jnp.int32), axis=2).astype(
        jnp.bfloat16
    )
    outgoing = jnp.dot(placing, tokens, preferred_element_type=jnp.float32).astype(jnp.bfloat16)
    outgoing = outgoing.reshape(n_experts, most, width)
    arrived = lax.all_to_all(outgoing, "expert", split_axis=0, concat_axis=0, tiled=True).reshape(
        slots_all, width
    )
    produced = expert_rows(
        arrived,
        lax.all_gather(w_gate, "dp", axis=2, tiled=True)[0],
        lax.all_gather(w_up, "dp", axis=2, tiled=True)[0],
        lax.all_gather(w_down, "dp", axis=2, tiled=True)[0],
    )
    answer = produced.astype(jnp.bfloat16).reshape(n_experts, most, width)
    back = lax.all_to_all(answer, "expert", split_axis=0, concat_axis=0, tiled=True).reshape(
        slots_all, width
    )
    picked = back[send_slot].astype(jnp.float32) * weight[:, None]
    mixed = jnp.sum(picked.reshape(tok_rows, 2, width), axis=1)
    return mixed.astype(jnp.bfloat16)


def solution(mesh):
    return jax.shard_map(
        local,
        mesh=mesh,
        in_specs=(
            P(("dp", "expert"), None),
            P(("dp", "expert"), None),
            P(("dp", "expert"), None),
            P(),
            P("expert", None, "dp"),
            P("expert", None, "dp"),
            P("expert", None, "dp"),
        ),
        out_specs=P(("dp", "expert"), None),
        check_vma=False,
    )
```

profile of v0, /device:TPU:0, one launch (start us, length us, event | category | flops | bytes accessed | tf_op | source)
XLA Modules:
  0.0 275.7 jit_solution(2728513415111079550)
XLA Ops:
  6.5 0.7 all-gather.5.cloned.1.call-update
  7.3 0.7 all-gather.7.cloned.1.call-update
  8.1 0.7 all-gather.9.cloned.1.call-update
  8.8 0.1 copy.23
  8.9 0.1 eq.39
  9.1 0.1 eq.43
  9.2 0.1 convert_reduce_fusion.1
  9.3 0.2 dynamic-update-slice
  9.6 42.6 %all-reduce = s32[256]{0:T(256)S(1)} all-reduce(s32[256]{0:T(256)S(1)} %dynamic-update-slice), channel_id=2, replica_groups=mesh['dp'=4,'expert'=8] {'dp','expert'}, use_global_device_ids=true, to_apply=%add | all-reduce | flops 256 | bytes 2048
  52.1 0.1 reshape.134
  52.2 0.6 reduce-window.6
  52.8 0.2 slice_reduce_fusion
  53.1 1.3 while.14
  54.4 0.1 select_reduce_fusion.1
  54.5 0.1 reduce_sum.63
  54.7 0.2 reduce_sum.66
  54.8 0.1 copy.27
  54.9 0.2 reduce_sum.68
  55.1 0.1 copy.29
  55.3 0.5 convolution_convert_fusion
  55.8 35.6 %all_to_all.10 = bf16[8,40,2048]{2,1,0:T(8,128)(2,1)S(1)} all-to-all(bf16[8,40,2048]{2,1,0:T(8,128)(2,1)S(1)} %bitcast.35), channel_id=1, replica_groups=mesh['dp'=4,'expert'=8] {'expert'}, dimensions={0} | all-to-all | bytes 2621440 | tf_op jit(solution)/shard_map/all_to_all | solution.py:55
  91.4 6.1 %fusion.4 = f32[320,1408]{1,0:T(8,128)} fusion(bf16[320,2048]{1,0:T(8,128)(2,1)S(1)} %bitcast.36, bf16[1,2048,1408]{1,2,0:T(8,128)(2,1)} %all-gather.5.cloned.1.call-done), kind=kOutput, calls=%fused_computation.7 | convolution fusion | flops 1845493760 | bytes 8880128 | tf_op jit(solution)/shard_map/dot_general | solution.py:21
  97.5 48.3 %all-gather.7.cloned.1.call-done = bf16[1,2048,1408]{1,2,0:T(8,128)(2,1)} async-done(((bf16[1,2048,352]{1,2,0:T(8,128)(2,1)}), bf16[1,2048,1408]{1,2,0:T(8,128)(2,1)}) %all-gather.7.cloned.1.call-update) | async-done | bytes 5767184 | tf_op jit(solution)/shard_map/all_gather | solution.py:61
  145.8 67.5 %all-gather.9.cloned.1.call-done = bf16[1,2048,1408]{1,2,0:T(8,128)(2,1)} async-done(((bf16[1,2048,352]{1,2,0:T(8,128)(2,1)}), bf16[1,2048,1408]{1,2,0:T(8,128)(2,1)}) %all-gather.9.cloned.1.call-update) | async-done | bytes 5767184 | tf_op jit(solution)/shard_map/all_gather | solution.py:62
  213.4 10.3 %fusion.9 = bf16[320,2048]{1,0:T(8,128)(2,1)} fusion(bf16[1,2048,1408]{1,2,0:T(8,128)(2,1)} %all-gather.9.cloned.1.call-done, bf16[320,2048]{1,0:T(8,128)(2,1)S(1)} %bitcast.37, bf16[1,2048,1408]{1,2,0:T(8,128)(2,1)} %all-gather.7.cloned.1.call-done, f32[320,1408]{1,0:T(8,128)} %fusion.4), kind=kOutput, calls=%fused_computation.10 | convolution fusion | flops 3694346240 | bytes 15958016 | tf_op jit(solution)/shard_map/dot_general | solution.py:24
  223.7 4.6 %all-to-all-start.1 = ((bf16[8,40,2048]{2,1,0:T(8,128)(2,1)}), bf16[8,40,2048]{2,1,0:T(8,128)(2,1)S(1)}, u32[]{:S(2)}, u32[]{:S(2)}) async-start(bf16[8,40,2048]{2,1,0:T(8,128)(2,1)} %bitcast.7), calls=%async_computation.1 | async-start | bytes 2621440 | tf_op jit(solution)/shard_map/all_to_all | solution.py:65
  228.3 0.1 mul.68
  228.4 0.1 copy.30
  228.5 31.9 %all-to-all-done.1 = bf16[8,40,2048]{2,1,0:T(8,128)(2,1)S(1)} async-done(((bf16[8,40,2048]{2,1,0:T(8,128)(2,1)}), bf16[8,40,2048]{2,1,0:T(8,128)(2,1)S(1)}, u32[]{:S(2)}, u32[]{:S(2)}) %all-to-all-start.1) | async-done | bytes 1310752 | tf_op jit(solution)/shard_map/all_to_all | solution.py:65
  260.5 2.3 gather_fusion
  262.8 2.4 reshape.125
  265.2 4.0 %multiply_reduce_fusion = bf16[128,2048]{1,0:T(8,128)(2,1)} fusion(f32[128,2,2048]{2,1,0:T(2,128)S(1)} %reshape.125, f32[128,2]{1,0:T(8,128)S(1)} %copy.30), kind=kLoop, calls=%fused_computation.13 | loop fusion | flops 786432 | bytes 2622464 | tf_op jit(solution)/shard_map/reduce_sum | solution.py:69
  (56 shorter events, 0.9 us)
Async XLA Ops:
  6.5 48.8 %copy-start = (bf16[128,2048]{1,0:T(8,128)(2,1)S(1)}, bf16[128,2048]{1,0:T(8,128)(2,1)}, u32[]{:S(2)}) copy-start(bf16[128,2048]{1,0:T(8,128)(2,1)} %param.9) | copy-start | bytes 1572868
  6.5 84.9 %all-gather.5.cloned.1.call-start = ((), (), s32[]{:S(2)}) async-start(), calls=%async_computation.2 | async-start | bytes 7208960 | tf_op jit(solution)/shard_map/all_gather | solution.py:60
  7.3 1.5 copy-start.1
  7.3 47.1 %copy-start.3 = (s32[8]{0:T(128)S(1)}, s32[8]{0:T(128)}, u32[]{:S(2)}) copy-start(s32[8]{0:T(128)} %param.12) | copy-start | bytes 100
  7.3 47.9 %copy-start.2 = (s32[128,2]{0,1:T(2,128)S(1)}, s32[128,2]{0,1:T(2,128)}, u32[]{:S(2)}) copy-start(s32[128,2]{0,1:T(2,128)} %param.11) | copy-start | bytes 3076
  7.3 138.6 %all-gather.7.cloned.1.call-start = ((), (), s32[]{:S(2)}) async-start(), calls=%async_computation.3 | async-start | bytes 7208960 | tf_op jit(solution)/shard_map/all_gather | solution.py:61
  8.0 205.4 %all-gather.9.cloned.1.call-start = ((), (), s32[]{:S(2)}) async-start(), calls=%async_computation.4 | async-start | bytes 7208960 | tf_op jit(solution)/shard_map/all_gather | solution.py:62
  223.7 36.8 %all-to-all-start.1 = ((bf16[8,40,2048]{2,1,0:T(8,128)(2,1)}), bf16[8,40,2048]{2,1,0:T(8,128)(2,1)S(1)}, u32[]{:S(2)}, u32[]{:S(2)}) async-start(bf16[8,40,2048]{2,1,0:T(8,128)(2,1)} %bitcast.7), calls=%async_computation.1 | async-start | bytes 2621440 | tf_op jit(solution)/shard_map/all_to_all | solution.py:65
Sparse Core Ops, SparseCore 0:
  9.2 69.0 all-gather.4
  80.1 65.6 all-gather.6
  147.7 65.6 all-gather.8
where the time goes:
time: 276 us
  waiting for transfers between devices  150 us (54%)
  blocking collectives  78.1 us (28%)
  matrix products  16.9 us (6%)
  between operations  13.3 us (5%)
  local copies, waits for them, and re-layouts  6.6 us (2%)
  other arithmetic  5.55 us (2%)
  starting transfers between devices  4.68 us (2%)
    all_gather x1, waiting for transfers between devices, local(): lax.all_gather(w_down, 'dp', axis=2, tiled=True)[0]  67.5 us
    all_gather x1, waiting for transfers between devices, local(): lax.all_gather(w_up, 'dp', axis=2, tiled=True)[0]  48.3 us
    unnamed x1, blocking collectives  42.6 us
    all_to_all x1, blocking collectives, local(): lax.all_to_all(outgoing, 'expert', split_axis=0, concat_axis=0, tiled=True)  35.6 us
    all_to_all x1, waiting for transfers between devices, local(): lax.all_to_all(answer, 'expert', split_axis=0, concat_axis=0, tiled=True)  31.9 us
    dot_general x1, matrix products, expert_rows(): lax.dot_general(hidden, down_w, (((1,), (1,)), ((), ())), preferred_eleme...  10.3 us
    dot_general x1, matrix products, expert_rows(): gate = jnp.dot(rows, gate_w, preferred_element_type=jnp.float32)  6.11 us
  transfers between devices with their start and end apart: 4, of which 3 were waited for; matrix products, arithmetic and copies ran while one was open for 4% of the time, Pallas kernels for 0%

commit v1 on v0

v1 whole, which is shorter than its diff:
```python
import functools

import jax
import jax.numpy as jnp
from jax import lax
from jax.experimental import pallas as pl
from jax.experimental.pallas import tpu as pltpu
from jax.sharding import PartitionSpec as P

MESH = pl.DeviceIdType.MESH


def exchange(
    n, out_ref, wg_ref, wu_ref, wd_ref, back_ref,
    xin, part, got1, sums, got2, ans,
    zs, zr, as_, ar, bs, br, cs, cr, ds, dr, es, er, loc,
):
    d = lax.axis_index("dp")
    e = lax.axis_index("expert")
    across = d + 1 - 2 * lax.rem(d, 2)
    along = lax.rem(d + 2, 4)
    most, half = xin.shape[3], xin.shape[4]
    near = ((across, e), (along, e))

    def remote(src, dst, send, recv, device):
        return pltpu.make_async_remote_copy(
            src_ref=src, dst_ref=dst, send_sem=send, recv_sem=recv,
            device_id=device, device_id_type=MESH,
        )

    def ahead(k):
        return (d, lax.rem(e + k, n))

    def behind(k):
        return (d, lax.rem(e + n - k, n))

    def to_owner(k):
        target = ahead(k)
        return remote(out_ref.at[target[1]], xin.at[k, 0], zs.at[k], zr.at[k], target)

    def spread(i, r):
        return remote(xin.at[i, 0], xin.at[i, 1 + r], as_.at[i, r], ar.at[i, r], near[r])

    def relay(i, r):
        return remote(
            xin.at[i, 1 + r, r], xin.at[i, 3, r], bs.at[i, r], br.at[i, r], near[1 - r]
        )

    def first(i, r):
        return remote(
            part.at[i, r, pl.ds(0, 2)], got1.at[i, r], cs.at[i, r], cr.at[i, r], near[r]
        )

    def second(i, r):
        return remote(sums.at[i, r], got2.at[i, r], ds.at[i, r], dr.at[i, r], near[1 - r])

    def give_back(i):
        return remote(ans.at[i], back_ref.at[e], es.at[i], er.at[i], behind(i))

    barrier = pltpu.get_barrier_semaphore()

    def greet(k, carry):
        pl.semaphore_signal(barrier, inc=1, device_id=ahead(k), device_id_type=MESH)
        return carry

    lax.fori_loop(1, n, greet, 0)
    for r in range(2):
        pl.semaphore_signal(barrier, inc=1, device_id=near[r], device_id_type=MESH)
    pl.semaphore_wait(barrier, n + 1)

    def launch(k, carry):
        to_owner(k).start()
        return carry

    own = pltpu.make_async_copy(out_ref.at[e], xin.at[0, 0], loc.at[0])
    own.start()
    lax.fori_loop(1, n, launch, 0)
    own.wait()

    def stage_a(i):
        @pl.when(i > 0)
        def _():
            to_owner(i).wait_recv()

        for r in range(2):
            spread(i, r).start()

    def stage_b(i):
        for r in range(2):
            spread(i, r).wait_recv()
            relay(i, r).start()

    def stage_c(i):
        for r in range(2):
            relay(i, r).wait_recv()
        gate = up = None
        for h in range(2):
            rows = xin[i, :, h].reshape(4 * most, half)
            g = jnp.dot(rows, wg_ref[0, pl.ds(h * half, half), :], preferred_element_type=jnp.float32)
            u = jnp.dot(rows, wu_ref[0, pl.ds(h * half, half), :], preferred_element_type=jnp.float32)
            gate, up = (g, u) if h == 0 else (gate + g, up + u)
        hidden = (gate / (1.0 + jnp.exp(-gate)) * up).astype(jnp.bfloat16)
        for h in range(2):
            made = lax.dot_general(
                hidden, wd_ref[0, pl.ds(h * half, half), :], (((1,), (1,)), ((), ())),
                preferred_element_type=jnp.float32,
            )
            for slot, block in enumerate(((1, 3, 0, 2), (2, 3, 0, 1))[h]):
                part[i, h, slot] = made[block * most:(block + 1) * most].astype(jnp.bfloat16)
            first(i, h).start()

    def stage_d(i):
        for r in range(2):
            first(i, r).wait_recv()
            total = part[i, r, 3].astype(jnp.float32) + got1[i, r, 1].astype(jnp.float32)
            sums[i, r] = total.astype(jnp.bfloat16)
            second(i, r).start()

    def stage_e(i):
        for r in range(2):
            second(i, r).wait_recv()
            total = (
                part[i, r, 2].astype(jnp.float32)
                + got1[i, r, 0].astype(jnp.float32)
                + got2[i, r].astype(jnp.float32)
            )
            ans[i, r] = total.astype(jnp.bfloat16)

        @pl.when(i > 0)
        def _():
            give_back(i).start()

        @pl.when(i == 0)
        def _():
            kept_here = pltpu.make_async_copy(ans.at[0], back_ref.at[e], loc.at[0])
            kept_here.start()
            kept_here.wait()

    stages = (stage_a, stage_b, stage_c, stage_d, stage_e)

    def step(t, carry):
        for lag, stage in reversed(list(enumerate(stages))):
            @pl.when((t >= lag) & (t < n + lag))
            def _(stage=stage, lag=lag):
                stage(t - lag)
        return carry

    lax.fori_loop(0, n + len(stages) - 1, step, 0)

    def settle(i, carry):
        for r in range(2):
            spread(i, r).wait_send()
            relay(i, r).wait_send()
            first(i, r).wait_send()
            second(i, r).wait_send()

        @pl.when(i > 0)
        def _():
            to_owner(i).wait_send()
            give_back(i).wait()

        return carry

    lax.fori_loop(0, n, settle, 0)


def experts(outgoing, w_gate, w_up, w_down):
    n, _, most, half = outgoing.shape
    bf16 = jnp.bfloat16
    vmem = pl.BlockSpec(memory_space=pltpu.VMEM)
    dma = pltpu.SemaphoreType.DMA
    return pl.pallas_call(
        functools.partial(exchange, n),
        out_shape=jax.ShapeDtypeStruct(outgoing.shape, bf16),
        in_specs=[vmem] * 4,
        out_specs=vmem,
        scratch_shapes=[
            pltpu.VMEM((n, 4, 2, most, half), bf16),
            pltpu.VMEM((n, 2, 4, most, half), bf16),
            pltpu.VMEM((n, 2, 2, most, half), bf16),
            pltpu.VMEM((n, 2, most, half), bf16),
            pltpu.VMEM((n, 2, most, half), bf16),
            pltpu.VMEM((n, 2, most, half), bf16),
            dma((n,)), dma((n,)),
            dma((n, 2)), dma((n, 2)),
            dma((n, 2)), dma((n, 2)),
            dma((n, 2)), dma((n, 2)),
            dma((n, 2)), dma((n, 2)),
            dma((n,)), dma((n,)),
            dma((1,)),
        ],
        compiler_params=pltpu.CompilerParams(
            collective_id=0, has_side_effects=True, vmem_limit_bytes=60 * 1024 * 1024
        ),
    )(outgoing, w_gate, w_up, w_down)


def local(tokens, expert_ids, gate_units, capacity, w_gate, w_up, w_down):
    tok_rows, width = tokens.shape
    n_experts = capacity.shape[0]
    most = max(2, 5 * tok_rows // (2 * n_experts))
    most = -(-most // 8) * 8
    slots_all = n_experts * most
    half = width // 2
    flat = expert_ids.reshape(-1)
    onehot = (flat[:, None] == jnp.arange(n_experts, dtype=jnp.int32)[None, :]).astype(jnp.int32)
    local_rank = jnp.sum((jnp.cumsum(onehot, axis=0) - onehot) * onehot, axis=1)
    send_slot = flat * most + local_rank
    chosen = send_slot.reshape(tok_rows, 2)[:, :, None] == jnp.arange(slots_all, dtype=jnp.int32)
    placing = (chosen[:, 0] | chosen[:, 1]).astype(jnp.bfloat16)
    outgoing = jnp.stack(
        [
            lax.dot_general(
                placing, tokens[:, h * half:(h + 1) * half], (((0,), (0,)), ((), ())),
                preferred_element_type=jnp.float32,
            ).astype(jnp.bfloat16).reshape(n_experts, most, half)
            for h in range(2)
        ],
        axis=1,
    )
    back = experts(outgoing, w_gate, w_up, w_down)

    counts = jnp.sum(onehot, axis=0)
    everything = lax.all_gather(counts, ("dp", "expert"))
    here = lax.axis_index(("dp", "expert"))
    earlier = jnp.arange(everything.shape[0], dtype=jnp.int32)[:, None] < here
    offsets = jnp.sum(jnp.where(earlier, everything, 0), axis=0)
    room = jnp.sum(onehot * (capacity - offsets)[None, :], axis=1)
    kept = local_rank < room
    units = jnp.where(kept, gate_units.reshape(-1), 0).reshape(tok_rows, 2)
    placed = jnp.sum(jnp.where(chosen, units[:, :, None], 0), axis=1)
    low = placed % 8
    high = (placed - low).astype(jnp.bfloat16)
    low = low.astype(jnp.bfloat16)
    mixed = []
    for h in range(2):
        rows = back[:, h].reshape(slots_all, half)
        total = jnp.dot(high, rows, preferred_element_type=jnp.float32) + jnp.dot(
            low, rows, preferred_element_type=jnp.float32
        )
        mixed.append((total * (1.0 / 1024.0)).astype(jnp.bfloat16))
    return jnp.concatenate(mixed, axis=1)


def solution(mesh):
    return jax.shard_map(
        local,
        mesh=mesh,
        in_specs=(
            P(("dp", "expert"), None),
            P(("dp", "expert"), None),
            P(("dp", "expert"), None),
            P(),
            P("expert", None, "dp"),
            P("expert", None, "dp"),
            P("expert", None, "dp"),
        ),
        out_specs=P(("dp", "expert"), None),
        check_vma=False,
    )
```

time: 276 us -> 160 us (0.58)
  waiting for transfers between devices: 150 us -> 0 us
  Pallas kernels: 0 us -> 101 us
  blocking collectives: 78.1 us -> 42 us
  matrix products: 16.9 us -> 3.08 us
  between operations: 13.3 us -> 0.18 us
  starting transfers between devices: 4.68 us -> 0 us
    all_gather x3 -> x0, waiting for transfers between devices: 116 us -> none  [the longest x1 67.5 us: local(): lax.all_gather(w_down, 'dp', axis=2, tiled=True)[0]]
    pallas_call x0 -> x1, Pallas kernels: none -> 101 us  [experts(): pl.pallas_call(functools.partial(exchange, n), out_shape=jax.ShapeDtypeSt...]
    all_to_all x1 -> x0, blocking collectives: 35.6 us -> none  [local(): lax.all_to_all(outgoing, 'expert', split_axis=0, concat_axis=0, tiled=True)]
    all_to_all x1 -> x0, waiting for transfers between devices: 31.9 us -> none  [local(): lax.all_to_all(answer, 'expert', split_axis=0, concat_axis=0, tiled=True)]
    dot_general x3 -> x6, matrix products: 16.9 us -> 3.08 us  [the longest x2 1.6 us: local(): lax.dot_general(placing, tokens[:, h * half:(h + 1) * half], (((0,), (0,)...]
    unnamed x11 -> x17, local copies, waits for them, and re-layouts: 0.38 us -> 6.52 us
    all_to_all x1 -> x0, starting transfers between devices: 4.61 us -> none  [local(): lax.all_to_all(answer, 'expert', split_axis=0, concat_axis=0, tiled=True)]
    reduce_sum x3, other arithmetic: 4.18 us -> 0.24 us  [the longest x1 0.1 us: local(): room = jnp.sum(onehot * (capacity - offsets)[None, :], axis=1)]
  transfers between devices with their start and end apart: 4 -> 0, of which waited for: 3 -> 0; matrix products, arithmetic and copies ran while one was open for 4% -> 0% of each run, Pallas kernels for 0% -> 0%
where the time goes in v1:
time: 160 us
  Pallas kernels  101 us (63%)
  blocking collectives  42 us (26%)
  local copies, waits for them, and re-layouts  8.88 us (6%)
  other arithmetic  4.49 us (3%)
  matrix products  3.08 us (2%)
    pallas_call x1, Pallas kernels, experts(): pl.pallas_call(functools.partial(exchange, n), out_shape=jax.ShapeDtypeSt...  101 us
    unnamed x1, blocking collectives  42 us
    unnamed x17, local copies, waits for them, and re-layouts  6.52 us

profile of v1, /device:TPU:0, one launch (start us, length us, event | category | flops | bytes accessed | tf_op | source)
XLA Modules:
  0.0 159.7 jit_solution(13472018028352553759)
XLA Ops:
  0.0 0.8 copy.33
  0.8 0.1 eq.40
  1.0 0.1 convert_reduce_fusion
  1.1 0.2 dynamic-update-slice
  1.4 42.0 %all-reduce = s32[256]{0:T(256)S(1)} all-reduce(s32[256]{0:T(256)S(1)} %dynamic-update-slice), channel_id=2, replica_groups=mesh['dp'=4,'expert'=8] {'dp','expert'}, use_global_device_ids=true, to_apply=%add | all-reduce | flops 256 | bytes 2048
  43.3 0.1 reshape.41
  43.4 0.1 select_reduce_fusion.1
  43.5 0.7 sub.10
  44.2 0.1 eq.44
  44.3 0.6 reduce-window.6
  44.9 0.2 slice_reduce_fusion
  45.2 0.1 select_reduce_fusion.2
  45.3 0.1 reduce_sum.50
  45.4 0.1 copy.35
  45.5 0.7 multiply_add_fusion
  46.2 1.3 convolution_convert_fusion
  47.5 0.3 convolution_convert_fusion.1
  47.9 1.2 pad_maximum_fusion.out_ref
  49.1 0.6 copy-done
  49.7 1.6 copy.38.wg_ref
  51.3 1.6 copy.39.wu_ref
  52.9 1.6 copy.40.wd_ref
  54.4 101.1 %shard_map.73 = bf16[8,2,40,1024]{3,2,1,0:T(8,128)(2,1)} custom-call(bf16[8,2,40,1024]{3,2,1,0:T(8,128)(2,1)} %pad_maximum_fusion.out_ref, bf16[1,2048,352]{2,1,0:T(8,128)(2,1)} %copy.38.wg_ref, bf16[1,2048,352]{2,1,0:T(8,128)(2,1)} %copy.39.wu_ref, bf16[1,2048,352]{2,1,0:T(8,128)(2,1)} %copy.40.wd_ref), custom_call_target="tpu_custom_call" | custom-call | tf_op jit(solution)/shard_map/pallas_call | solution.py:172
  155.5 1.4 fusion.18
  156.9 0.1 copy.36
  157.1 0.1 reduce_sum.54
  157.2 0.1 copy.37
  157.3 0.4 fusion.16
  157.7 0.4 fusion.3
  158.1 0.4 fusion.17
  158.5 0.4 fusion.2
  158.8 0.8 pad_maximum_fusion.1
  (17 shorter events, 0.2 us)
Async XLA Ops:
  0.0 47.5 %copy-start.3 = (bf16[128,2048]{1,0:T(8,128)(2,1)S(1)}, bf16[128,2048]{1,0:T(8,128)(2,1)}, u32[]{:S(2)}) copy-start(bf16[128,2048]{1,0:T(8,128)(2,1)} %param.7) | copy-start | bytes 1572868
  47.9 1.8 %copy-start = (bf16[1,2048,352]{1,2,0:T(8,128)(2,1)S(1)}, bf16[1,2048,352]{1,2,0:T(8,128)(2,1)}, u32[]{:S(2)}) copy-start(bf16[1,2048,352]{1,2,0:T(8,128)(2,1)} %param.11) | copy-start | bytes 4325380
  49.7 1.6 copy-start.1
  51.3 1.6 copy-start.2
  155.5 1.4 copy-start.4

commit v2 on v1

v2 whole, which is shorter than its diff:
```python
import functools

import jax
import jax.numpy as jnp
from jax import lax
from jax.experimental import pallas as pl
from jax.experimental.pallas import tpu as pltpu
from jax.sharding import PartitionSpec as P

MESH = pl.DeviceIdType.MESH


def exchange(
    n, most, tok_ref, ids_ref, turned_ref, units_ref, cap_ref, wg_hbm, wu_hbm, wd_hbm, out_ref,
    wg_ref, wu_ref, wd_ref, outgoing, xin, part, got1, sums, got2, ans, back, acc, code, scale, table,
    zs, zr, as_, ar, bs, br, cs, cr, ds, dr, es, er, ks, kr, ts, tr, loc,
):
    d = lax.axis_index("dp")
    e = lax.axis_index("expert")
    across = d + 1 - 2 * lax.rem(d, 2)
    along = lax.rem(d + 2, 4)
    diagonal = lax.rem(across + 2, 4)
    half = xin.shape[4]
    tok_rows = tok_ref.shape[0]
    lanes = table.shape[3]
    near = ((across, e), (along, e))
    f32, bf16 = jnp.float32, jnp.bfloat16

    def remote(src, dst, send, recv, device):
        return pltpu.make_async_remote_copy(
            src_ref=src, dst_ref=dst, send_sem=send, recv_sem=recv,
            device_id=device, device_id_type=MESH,
        )

    def ahead(k):
        return (d, lax.rem(e + k, n))

    def behind(k):
        return (d, lax.rem(e + n - k, n))

    def to_owner(k):
        return remote(outgoing.at[k], xin.at[k, 0], zs.at[k], zr.at[k], ahead(k))

    def spread(i, r):
        return remote(xin.at[i, 0], xin.at[i, 1 + r], as_.at[i, r], ar.at[i, r], near[r])

    def relay(i, r):
        return remote(
            xin.at[i, 1 + r, r], xin.at[i, 3, r], bs.at[i, r], br.at[i, r], near[1 - r]
        )

    def first(i, r):
        return remote(
            part.at[i, r, pl.ds(0, 2)], got1.at[i, r], cs.at[i, r], cr.at[i, r], near[r]
        )

    def second(i, r):
        return remote(sums.at[i, r], got2.at[i, r], ds.at[i, r], dr.at[i, r], near[1 - r])

    def give_back(i):
        return remote(ans.at[i], back.at[i], es.at[i], er.at[i], behind(i))

    def count_out(k):
        return remote(table.at[0, 0], table.at[0, k], ks.at[k], kr.at[k], ahead(k))

    def table_near(r):
        return remote(table.at[0], table.at[1 + r], ts.at[r], tr.at[r], near[r])

    def table_far():
        return remote(table.at[1], table.at[3], ts.at[2], tr.at[2], near[1])

    def weights():
        return [
            pltpu.make_async_copy(hbm.at[0], vmem, loc.at[1 + w])
            for w, (hbm, vmem) in enumerate(((wg_hbm, wg_ref), (wu_hbm, wu_ref), (wd_hbm, wd_ref)))
        ]

    barrier = pltpu.get_barrier_semaphore()

    def greet(k, carry):
        pl.semaphore_signal(barrier, inc=1, device_id=ahead(k), device_id_type=MESH)
        return carry

    lax.fori_loop(1, n, greet, 0)
    for r in range(2):
        pl.semaphore_signal(barrier, inc=1, device_id=near[r], device_id_type=MESH)
    for copy in weights():
        copy.start()

    def iota(shape, axis):
        return lax.broadcasted_iota(jnp.int32, shape, axis)

    square = (tok_rows, tok_rows)
    ids = ids_ref[...]
    hot = [(iota((tok_rows, lanes), 1) == ids[:, k:k + 1]) for k in range(2)]
    named = jnp.where(hot[0] | hot[1], 1.0, 0.0)
    table[0, 0] = jnp.sum(named, axis=0, keepdims=True).astype(jnp.int32)
    lower = jnp.where(iota(square, 1) < iota(square, 0), 1.0, 0.0).astype(bf16)
    before = jnp.dot(lower, named.astype(bf16), preferred_element_type=f32)
    rank = [jnp.sum(jnp.where(h, before, 0.0), axis=1, keepdims=True) for h in hot]
    for k in range(2):
        slot = ids[:, k:k + 1] * most + rank[k].astype(jnp.int32)
        code[k] = jnp.broadcast_to(slot, (tok_rows, most))

    turned = turned_ref[...]
    hot_t = [(iota((n, tok_rows), 0) == turned[k:k + 1, :]) for k in range(2)]
    named_t = jnp.where(hot_t[0] | hot_t[1], 1.0, 0.0).astype(bf16)
    upper = jnp.where(iota(square, 0) < iota(square, 1), 1.0, 0.0).astype(bf16)
    before_t = jnp.dot(named_t, upper, preferred_element_type=f32)
    code_t = [
        turned[k:k + 1, :] * most
        + jnp.sum(jnp.where(hot_t[k], before_t, 0.0), axis=0, keepdims=True).astype(jnp.int32)
        for k in range(2)
    ]

    def rows_for(p, h):
        wanted = iota((most, tok_rows), 0) + p * most
        placing = jnp.where((code_t[0] == wanted) | (code_t[1] == wanted), 1.0, 0.0).astype(bf16)
        return jnp.dot(
            placing, tok_ref[:, h * half:(h + 1) * half], preferred_element_type=f32
        ).astype(bf16)

    for h in range(2):
        xin[0, 0, h] = rows_for(e, h)

    pl.semaphore_wait(barrier, n + 1)

    def counted(k, carry):
        count_out(k).start()
        return carry

    def launch(k, carry):
        for h in range(2):
            outgoing[k, h] = rows_for(ahead(k)[1], h)
        to_owner(k).start()
        return carry

    for r in range(2):
        spread(0, r).start()
    lax.fori_loop(1, n, counted, 0)
    lax.fori_loop(1, n, launch, 0)
    acc[...] = jnp.zeros_like(acc)

    def stage_a(i):
        @pl.when(i > 0)
        def _():
            to_owner(i).wait_recv()
            for r in range(2):
                spread(i, r).start()

    def stage_b(i):
        for r in range(2):
            spread(i, r).wait_recv()
            relay(i, r).start()

    def stage_c(i):
        @pl.when(i == 0)
        def _():
            for copy in weights():
                copy.wait()

        for r in range(2):
            relay(i, r).wait_recv()
        gate = up = None
        for h in range(2):
            rows = xin[i, :, h].reshape(4 * most, half)
            g = jnp.dot(rows, wg_ref[pl.ds(h * half, half), :], preferred_element_type=f32)
            u = jnp.dot(rows, wu_ref[pl.ds(h * half, half), :], preferred_element_type=f32)
            gate, up = (g, u) if h == 0 else (gate + g, up + u)
        hidden = (gate / (1.0 + jnp.exp(-gate)) * up).astype(bf16)
        for h in range(2):
            made = lax.dot_general(
                hidden, wd_ref[pl.ds(h * half, half), :], (((1,), (1,)), ((), ())),
                preferred_element_type=f32,
            )
            for slot, block in enumerate(((1, 3, 0, 2), (2, 3, 0, 1))[h]):
                part[i, h, slot] = made[block * most:(block + 1) * most].astype(bf16)
            first(i, h).start()

    def stage_d(i):
        for r in range(2):
            first(i, r).wait_recv()
            total = part[i, r, 3].astype(f32) + got1[i, r, 1].astype(f32)
            sums[i, r] = total.astype(bf16)
            second(i, r).start()

    def stage_e(i):
        for r in range(2):
            second(i, r).wait_recv()
            total = (
                part[i, r, 2].astype(f32) + got1[i, r, 0].astype(f32) + got2[i, r].astype(f32)
            )
            ans[i, r] = total.astype(bf16)

        @pl.when(i > 0)
        def _():
            give_back(i).start()

        @pl.when(i == 0)
        def _():
            kept_here = pltpu.make_async_copy(ans.at[0], back.at[0], loc.at[0])
            kept_here.start()
            kept_here.wait()

    def stage_f(i):
        @pl.when(i > 0)
        def _():
            give_back(i).wait_recv()

        wanted = iota((tok_rows, most), 1) + ahead(i)[1] * most
        placed = jnp.where(code[0] == wanted, scale[0], 0) + jnp.where(code[1] == wanted, scale[1], 0)
        low = placed & 7
        high = (placed - low).astype(f32).astype(bf16)
        low = low.astype(f32).astype(bf16)
        for h in range(2):
            rows = back[i, h]
            acc[:, h * half:(h + 1) * half] += jnp.dot(
                high, rows, preferred_element_type=f32
            ) + jnp.dot(low, rows, preferred_element_type=f32)

    def counts_near():
        def arrived(k, carry):
            count_out(k).wait_recv()
            return carry

        lax.fori_loop(1, n, arrived, 0)
        for r in range(2):
            table_near(r).start()

    def counts_far():
        for r in range(2):
            table_near(r).wait_recv()
        table_far().start()

    def counts_used():
        table_far().wait_recv()
        here = d * n + e
        offsets = jnp.zeros((1, lanes), jnp.int32)
        for s, row in enumerate((d, across, along, diagonal)):
            def add(k, total, s=s, row=row):
                earlier = row * n + behind(k)[1] < here
                return total + table[s, k] * earlier.astype(jnp.int32)

            offsets = lax.fori_loop(0, n, add, offsets)
        room = (cap_ref[...] - offsets).astype(f32)
        for k in range(2):
            limit = jnp.sum(jnp.where(hot[k], room, 0.0), axis=1, keepdims=True)
            units = jnp.where(rank[k] < limit, units_ref[:, k:k + 1], 0)
            scale[k] = jnp.broadcast_to(units, (tok_rows, most))

    stages = ((0, stage_a), (2, stage_b), (4, stage_c), (6, stage_d), (8, stage_e), (10, stage_f))

    def step(t, carry):
        for lag, stage in stages:
            @pl.when((t >= lag) & (t < n + lag))
            def _(stage=stage, lag=lag):
                stage(t - lag)
        for when, chore in ((3, counts_near), (5, counts_far), (7, counts_used)):
            pl.when(t == when)(chore)
        return carry

    lax.fori_loop(0, n + stages[-1][0], step, 0)
    out_ref[...] = (acc[...] * (1.0 / 1024.0)).astype(out_ref.dtype)

    def settle(i, carry):
        for r in range(2):
            spread(i, r).wait_send()
            relay(i, r).wait_send()
            first(i, r).wait_send()
            second(i, r).wait_send()

        @pl.when(i > 0)
        def _():
            to_owner(i).wait_send()
            give_back(i).wait_send()
            count_out(i).wait_send()

        return carry

    lax.fori_loop(0, n, settle, 0)
    for r in range(2):
        table_near(r).wait_send()
    table_far().wait_send()


def local(tokens, expert_ids, gate_units, capacity, w_gate, w_up, w_down):
    tok_rows, width = tokens.shape
    n = capacity.shape[0]
    most = max(2, 5 * tok_rows // (2 * n))
    most = -(-most // 8) * 8
    half = width // 2
    lanes = -(-n // 128) * 128
    bf16 = jnp.bfloat16
    vmem = pl.BlockSpec(memory_space=pltpu.VMEM)
    hbm = pl.BlockSpec(memory_space=pl.ANY)
    dma = pltpu.SemaphoreType.DMA
    block = (most, half)
    return pl.pallas_call(
        functools.partial(exchange, n, most),
        out_shape=jax.ShapeDtypeStruct(tokens.shape, bf16),
        in_specs=[vmem] * 5 + [hbm] * 3,
        out_specs=vmem,
        scratch_shapes=[
            pltpu.VMEM(w_gate.shape[1:], bf16),
            pltpu.VMEM(w_up.shape[1:], bf16),
            pltpu.VMEM(w_down.shape[1:], bf16),
            pltpu.VMEM((n, 2) + block, bf16),
            pltpu.VMEM((n, 4, 2) + block, bf16),
            pltpu.VMEM((n, 2, 4) + block, bf16),
            pltpu.VMEM((n, 2, 2) + block, bf16),
            pltpu.VMEM((n, 2) + block, bf16),
            pltpu.VMEM((n, 2) + block, bf16),
            pltpu.VMEM((n, 2) + block, bf16),
            pltpu.VMEM((n, 2) + block, bf16),
            pltpu.VMEM((tok_rows, width), jnp.float32),
            pltpu.VMEM((2, tok_rows, most), jnp.int32),
            pltpu.VMEM((2, tok_rows, most), jnp.int32),
            pltpu.VMEM((4, n, 1, lanes), jnp.int32),
            dma((n,)), dma((n,)),
            dma((n, 2)), dma((n, 2)),
            dma((n, 2)), dma((n, 2)),
            dma((n, 2)), dma((n, 2)),
            dma((n, 2)), dma((n, 2)),
            dma((n,)), dma((n,)),
            dma((n,)), dma((n,)),
            dma((3,)), dma((3,)),
            dma((4,)),
        ],
        compiler_params=pltpu.CompilerParams(
            collective_id=0, has_side_effects=True, vmem_limit_bytes=60 * 1024 * 1024
        ),
    )(
        tokens, expert_ids, expert_ids.T, gate_units,
        jnp.pad(capacity, (0, lanes - n))[None, :], w_gate, w_up, w_down,
    )


def solution(mesh):
    return jax.shard_map(
        local,
        mesh=mesh,
        in_specs=(
            P(("dp", "expert"), None),
            P(("dp", "expert"), None),
            P(("dp", "expert"), None),
            P(),
            P("expert", None, "dp"),
            P("expert", None, "dp"),
            P("expert", None, "dp"),
        ),
        out_specs=P(("dp", "expert"), None),
        check_vma=False,
    )
```

time: 160 us -> 128 us (0.80)
  blocking collectives: 42 us -> 0 us
  Pallas kernels: 101 us -> 116 us
  other arithmetic: 4.49 us -> 0 us
  matrix products: 3.08 us -> 0 us
  local copies, waits for them, and re-layouts: 8.88 us -> 11.7 us
    unnamed x1 -> x0, blocking collectives: 42 us -> none
    pallas_call x1, Pallas kernels: 101 us -> 116 us  [local(): pl.pallas_call(functools.partial(exchange, n, most), out_shape=jax.ShapeD...]
    unnamed x17 -> x10, local copies, waits for them, and re-layouts: 6.52 us -> 10.5 us
    dot_general x6 -> x0, matrix products: 3.08 us -> none  [the longest x2 1.6 us: local(): lax.dot_general(placing, tokens[:, h * half:(h + 1) * half], (((0,), (0,)...]
    another operation x3 -> x0, other arithmetic: 1.85 us -> none  [the longest x1 1.22 us: local(): jnp.stack([lax.dot_general(placing, tokens[:, h * half:(h + 1) * half], (...]
    slice x2 -> x0, local copies, waits for them, and re-layouts: 1.61 us -> none  [the longest x1 1.39 us: local(): rows = back[:, h].reshape(slots_all, half)]
where the time goes in v2:
time: 128 us
  Pallas kernels  116 us (91%)
  local copies, waits for them, and re-layouts  11.7 us (9%)
    pallas_call x1, Pallas kernels, local(): pl.pallas_call(functools.partial(exchange, n, most), out_shape=jax.ShapeD...  116 us
    unnamed x10, local copies, waits for them, and re-layouts  10.5 us

profile of v2, /device:TPU:0, one launch (start us, length us, event | category | flops | bytes accessed | tf_op | source)
XLA Modules:
  0.0 127.8 jit_solution(7669092295130604202)
XLA Ops:
  0.0 1.2 pad_bitcast_fusion.cap_ref
  1.2 0.0 copy-start
  1.2 1.5 %copy.9.units_ref = s32[128,2]{1,0:T(8,128)} copy(s32[128,2]{0,1:T(2,128)} %param.9) | data formatting | bytes 2048 | tf_op args[2]
  2.7 1.4 %copy.8.ids_ref = s32[128,2]{1,0:T(8,128)} copy(s32[128,2]{0,1:T(2,128)} %param.8) | data formatting | bytes 2048 | tf_op args[1]
  4.1 2.6 %copy.10.wg_hbm = bf16[1,2048,352]{2,1,0:T(8,128)(2,1)} copy(bf16[1,2048,352]{1,2,0:T(8,128)(2,1)} %param.11) | data formatting | bytes 2883584 | tf_op args[4]
  6.7 0.0 copy-done
  6.7 0.0 copy-start.1
  6.7 1.6 %copy.11.wu_hbm = bf16[1,2048,352]{2,1,0:T(8,128)(2,1)} copy(bf16[1,2048,352]{1,2,0:T(8,128)(2,1)S(1)} %copy-done) | data formatting | bytes 2883584 | tf_op args[5]
  8.2 0.0 copy-done.1
  8.2 1.6 %copy.12.wd_hbm = bf16[1,2048,352]{2,1,0:T(8,128)(2,1)} copy(bf16[1,2048,352]{1,2,0:T(8,128)(2,1)S(1)} %copy-done.1) | data formatting | bytes 2883584 | tf_op args[6]
  9.8 116.1 %shard_map.73 = bf16[128,2048]{1,0:T(8,128)(2,1)} custom-call(bf16[128,2048]{1,0:T(8,128)(2,1)} %tok_ref.1, s32[128,2]{1,0:T(8,128)} %copy.8.ids_ref, s32[2,128]{1,0:T(2,128)} %bitcast.3, s32[128,2]{1,0:T(8,128)} %copy.9.units_ref, s32[1,128]{1,0:T(1,128)} %pad_bitcast_fusion.cap_ref, bf16[1,2048,352]{2,1,0:T(8,128)(2,1)} %copy.10.wg_hbm, ...), custom_call_target="tpu_custom_call" | custom-call | tf_op jit(solution)/shard_map/pallas_call | solution.py:298
  125.9 1.9 %copy.14 = bf16[128,2048]{1,0:T(8,128)(2,1)} copy(bf16[128,2048]{1,0:T(8,128)(2,1)} %shard_map.73) | data formatting | bytes 1048576
Async XLA Ops:
  1.2 5.5 %copy-start = (bf16[1,2048,352]{1,2,0:T(8,128)(2,1)S(1)}, bf16[1,2048,352]{1,2,0:T(8,128)(2,1)}, u32[]{:S(2)}) copy-start(bf16[1,2048,352]{1,2,0:T(8,128)(2,1)} %param.12) | copy-start | bytes 4325380
  6.7 1.6 %copy-start.1 = (bf16[1,2048,352]{1,2,0:T(8,128)(2,1)S(1)}, bf16[1,2048,352]{1,2,0:T(8,128)(2,1)}, u32[]{:S(2)}) copy-start(bf16[1,2048,352]{1,2,0:T(8,128)(2,1)} %param.13) | copy-start | bytes 4325380

commit v3 on v2

--- a/solution.py
+++ b/solution.py
@@ -11,8 +11,8 @@
 
 
 def exchange(
-    n, most, tok_ref, ids_ref, turned_ref, units_ref, cap_ref, wg_hbm, wu_hbm, wd_hbm, out_ref,
-    wg_ref, wu_ref, wd_ref, outgoing, xin, part, got1, sums, got2, ans, back, acc, code, scale, table,
+    n, most, tok_ref, turned_ref, units_ref, cap_ref, wg_hbm, wu_hbm, wd_hbm, out_ref,
+    wgu_ref, wd_ref, outgoing, xin, part, got1, sums, got2, ans, back, acc, code, scale, table,
     zs, zr, as_, ar, bs, br, cs, cr, ds, dr, es, er, ks, kr, ts, tr, loc,
 ):
     d = lax.axis_index("dp")
@@ -23,6 +23,7 @@
     half = xin.shape[4]
     tok_rows = tok_ref.shape[0]
     lanes = table.shape[3]
+    hidden_units = wd_ref.shape[0]
     near = ((across, e), (along, e))
     f32, bf16 = jnp.float32, jnp.bfloat16
 
@@ -70,9 +71,13 @@
         return remote(table.at[1], table.at[3], ts.at[2], tr.at[2], near[1])
 
     def weights():
+        pairs = (
+            (wg_hbm, wgu_ref.at[pl.ds(0, hidden_units)]),
+            (wu_hbm, wgu_ref.at[pl.ds(hidden_units, hidden_units)]),
+            (wd_hbm, wd_ref),
+        )
         return [
-            pltpu.make_async_copy(hbm.at[0], vmem, loc.at[1 + w])
-            for w, (hbm, vmem) in enumerate(((wg_hbm, wg_ref), (wu_hbm, wu_ref), (wd_hbm, wd_ref)))
+            pltpu.make_async_copy(hbm, vmem, loc.at[1 + w]) for w, (hbm, vmem) in enumerate(pairs)
         ]
 
     barrier = pltpu.get_barrier_semaphore()
@@ -91,18 +96,22 @@
         return lax.broadcasted_iota(jnp.int32, shape, axis)
 
     square = (tok_rows, tok_rows)
-    ids = ids_ref[...]
-    hot = [(iota((tok_rows, lanes), 1) == ids[:, k:k + 1]) for k in range(2)]
+    turned = turned_ref[...]
+
+    def upright(row):
+        return jnp.broadcast_to(row, square).T[:, :1]
+
+    ids = [upright(turned[k:k + 1, :]) for k in range(2)]
+    hot = [(iota((tok_rows, lanes), 1) == ids[k]) for k in range(2)]
     named = jnp.where(hot[0] | hot[1], 1.0, 0.0)
     table[0, 0] = jnp.sum(named, axis=0, keepdims=True).astype(jnp.int32)
     lower = jnp.where(iota(square, 1) < iota(square, 0), 1.0, 0.0).astype(bf16)
     before = jnp.dot(lower, named.astype(bf16), preferred_element_type=f32)
     rank = [jnp.sum(jnp.where(h, before, 0.0), axis=1, keepdims=True) for h in hot]
     for k in range(2):
-        slot = ids[:, k:k + 1] * most + rank[k].astype(jnp.int32)
+        slot = ids[k] * most + rank[k].astype(jnp.int32)
         code[k] = jnp.broadcast_to(slot, (tok_rows, most))
 
-    turned = turned_ref[...]
     hot_t = [(iota((n, tok_rows), 0) == turned[k:k + 1, :]) for k in range(2)]
     named_t = jnp.where(hot_t[0] | hot_t[1], 1.0, 0.0).astype(bf16)
     upper = jnp.where(iota(square, 0) < iota(square, 1), 1.0, 0.0).astype(bf16)
@@ -161,17 +170,19 @@
 
         for r in range(2):
             relay(i, r).wait_recv()
-        gate = up = None
+        both = None
         for h in range(2):
             rows = xin[i, :, h].reshape(4 * most, half)
-            g = jnp.dot(rows, wg_ref[pl.ds(h * half, half), :], preferred_element_type=f32)
-            u = jnp.dot(rows, wu_ref[pl.ds(h * half, half), :], preferred_element_type=f32)
-            gate, up = (g, u) if h == 0 else (gate + g, up + u)
+            term = lax.dot_general(
+                rows, wgu_ref[:, h * half:(h + 1) * half], (((1,), (1,)), ((), ())),
+                preferred_element_type=f32,
+            )
+            both = term if h == 0 else both + term
+        gate, up = both[:, :hidden_units], both[:, hidden_units:]
         hidden = (gate / (1.0 + jnp.exp(-gate)) * up).astype(bf16)
         for h in range(2):
-            made = lax.dot_general(
-                hidden, wd_ref[pl.ds(h * half, half), :], (((1,), (1,)), ((), ())),
-                preferred_element_type=f32,
+            made = jnp.dot(
+                hidden, wd_ref[:, h * half:(h + 1) * half], preferred_element_type=f32
             )
             for slot, block in enumerate(((1, 3, 0, 2), (2, 3, 0, 1))[h]):
                 part[i, h, slot] = made[block * most:(block + 1) * most].astype(bf16)
@@ -242,13 +253,18 @@
                 return total + table[s, k] * earlier.astype(jnp.int32)
 
             offsets = lax.fori_loop(0, n, add, offsets)
-        room = (cap_ref[...] - offsets).astype(f32)
+        most_taken = lax.fori_loop(
+            0, n,
+            lambda j, row: jnp.where(iota((1, lanes), 1) == j, cap_ref[j], row),
+            jnp.zeros((1, lanes), jnp.int32),
+        )
+        room = (most_taken - offsets).astype(f32)
         for k in range(2):
             limit = jnp.sum(jnp.where(hot[k], room, 0.0), axis=1, keepdims=True)
-            units = jnp.where(rank[k] < limit, units_ref[:, k:k + 1], 0)
+            units = jnp.where(rank[k] < limit, upright(units_ref[k:k + 1, :]), 0)
             scale[k] = jnp.broadcast_to(units, (tok_rows, most))
 
-    stages = ((0, stage_a), (2, stage_b), (4, stage_c), (6, stage_d), (8, stage_e), (10, stage_f))
+    stages = ((0, stage_a), (2, stage_b), (6, stage_d), (8, stage_e), (4, stage_c), (10, stage_f))
 
     def step(t, carry):
         for lag, stage in stages:
@@ -298,12 +314,11 @@
     return pl.pallas_call(
         functools.partial(exchange, n, most),
         out_shape=jax.ShapeDtypeStruct(tokens.shape, bf16),
-        in_specs=[vmem] * 5 + [hbm] * 3,
+        in_specs=[vmem] * 3 + [pl.BlockSpec(memory_space=pltpu.SMEM)] + [hbm] * 3,
         out_specs=vmem,
         scratch_shapes=[
-            pltpu.VMEM(w_gate.shape[1:], bf16),
-            pltpu.VMEM(w_up.shape[1:], bf16),
-            pltpu.VMEM(w_down.shape[1:], bf16),
+            pltpu.VMEM((2 * w_gate.shape[2], width), bf16),
+            pltpu.VMEM((w_down.shape[2], width), bf16),
             pltpu.VMEM((n, 2) + block, bf16),
             pltpu.VMEM((n, 4, 2) + block, bf16),
             pltpu.VMEM((n, 2, 4) + block, bf16),
@@ -330,8 +345,7 @@
             collective_id=0, has_side_effects=True, vmem_limit_bytes=60 * 1024 * 1024
         ),
     )(
-        tokens, expert_ids, expert_ids.T, gate_units,
-        jnp.pad(capacity, (0, lanes - n))[None, :], w_gate, w_up, w_down,
+        tokens, expert_ids.T, gate_units.T, capacity, w_gate[0].T, w_up[0].T, w_down[0].T,
     )
 
 

time: 128 us -> 118 us (0.922)
  local copies, waits for them, and re-layouts: 11.7 us -> 1.88 us
    unnamed x10 -> x1, local copies, waits for them, and re-layouts: 10.5 us -> 1.88 us
where the time goes in v3:
time: 118 us
  Pallas kernels  116 us (98%)
  local copies, waits for them, and re-layouts  1.88 us (2%)
    pallas_call x1, Pallas kernels, local(): pl.pallas_call(functools.partial(exchange, n, most), out_shape=jax.ShapeD...  116 us

profile of v3, /device:TPU:0, one launch (start us, length us, event | category | flops | bytes accessed | tf_op | source)
XLA Modules:
  0.0 118.0 jit_solution(15106213496121152039)
XLA Ops:
  0.0 116.1 %shard_map.73 = bf16[128,2048]{1,0:T(8,128)(2,1)} custom-call(bf16[128,2048]{1,0:T(8,128)(2,1)} %tok_ref.1, s32[2,128]{1,0:T(2,128)} %bitcast.14, s32[2,128]{1,0:T(2,128)} %bitcast.15, s32[8]{0:T(128)} %cap_ref.1, bf16[352,2048]{1,0:T(8,128)(2,1)} %bitcast.11, bf16[352,2048]{1,0:T(8,128)(2,1)} %bitcast.12, bf16[352,2048]{1,0:T(8,128)(2,1)} %bitcast.13), custom_call_target="tpu_custom_call" | custom-call | tf_op jit(solution)/shard_map/pallas_call | solution.py:314
  116.1 1.9 %copy.9 = bf16[128,2048]{1,0:T(8,128)(2,1)} copy(bf16[128,2048]{1,0:T(8,128)(2,1)} %shard_map.73) | data formatting | bytes 1048576
